TPU v7x, 1024 devices: a whole 4x4x32 slice. The times are simulated.
1024 devices in a mesh: ctx: 32 (over z), ep: 32 (over x, y, core).
Axes of the slice: x: 4, y: 4, z: 32, core: 2. Of those that a mesh axis runs over, the one named last changes fastest.
Arguments:
- out_grad: bfloat16 [2048, 3584], P(('ctx', 'ep')), may hold values from -6 to 6
- expert_ids: int32 [2048, 8], P(('ctx', 'ep')), may hold values from 0 to 127, all different within a row; in each aligned block of 64 rows (0 to 63, 64 to 127, ...) at most 7 rows name the same one
- gate_values: float32 [2048, 8], P(('ctx', 'ep')), may hold values from 0.1 to 2.5
- hidden: bfloat16 [32, 128, 7, 1536], P(None, 'ep', None, 'ctx'), may hold values from -0.29882812 to 0.29882812
- w_down: bfloat16 [128, 1536, 3584], P('ep', 'ctx'), may hold values from -0.15625 to 0.15625
Outputs:
- hidden_grad: bfloat16 [32, 128, 7, 1536], P(None, 'ep', None, 'ctx')
- weight_grad: bfloat16 [128, 1536, 3584], P('ep', 'ctx')
- gate_grad: float32 [2048, 8], P(('ctx', 'ep'))
Inputs may be any that keep to these rules, and one draw needn't show every extreme that they name: `expert_ids`: each token names 8 different experts. In each aligned block of 64 tokens no expert is named by more than 7 tokens.
All inputs are finite; a program needn't handle non-finite values.
Results may differ from a plain program's by a relative error of at most 0.012.
Values may be sent and summed in bfloat16 or wider, within the bound.
A program may use at most 64 MiB of HBM per device.

v0:
```python
import jax
import jax.numpy as jnp
from jax import lax
from jax.sharding import PartitionSpec as P


def from_everyone(value, axis):
    count = lax.axis_size(axis)
    return lax.all_to_all(
        jnp.broadcast_to(value[None], (count, *value.shape)), axis, 0, 0, tiled=True
    )


def in_order(pieces, dim):
    lengths = list(pieces.shape[1:])
    lengths[dim] *= pieces.shape[0]
    return jnp.moveaxis(pieces, 0, dim).reshape(lengths)


def collect(value, axis, dim):
    pieces = from_everyone(value, axis)
    return in_order(pieces, dim)


def cut_along(value, dim, count):
    before, after = (value.shape[:dim], value.shape[dim + 1 :])
    return jnp.moveaxis(value.reshape(*before, count, -1, *after), dim, 0)


def summed_on_arrival(value, axis, dim):
    count = lax.axis_size(axis)
    pieces = lax.all_to_all(cut_along(value, dim, count), axis, 0, 0, tiled=True)
    return jnp.sum(pieces, axis=0)


def route_places(group_ids, experts_all, capacity):
    flat_ids = group_ids.reshape(-1)
    onehot = (flat_ids[:, None] == jnp.arange(experts_all, dtype=jnp.int32)[None, :]).astype(
        jnp.int32
    )
    before = jnp.cumsum(onehot, axis=0) - onehot
    slot_index = jnp.sum(before * onehot, axis=1)
    return (flat_ids * capacity + slot_index).astype(jnp.int32)


def per_device(out_grad, expert_ids, gate_values, hidden, w_down):
    tok_dev, top_count = expert_ids.shape
    groups, exp_dev, capacity, width_part = hidden.shape
    model_width = out_grad.shape[1]
    ep_count = lax.axis_size("ep")
    ep_rank = lax.axis_index("ep")
    slots_dev = exp_dev * capacity
    experts_all = exp_dev * ep_count
    own_first = ep_rank * slots_dev
    slot_range = jnp.arange(slots_dev, dtype=jnp.int32)
    group_rows, group_ids, group_gates = (
        collect(out_grad, "ep", 0),
        collect(expert_ids, "ep", 0),
        collect(gate_values.astype(jnp.bfloat16), "ep", 0).astype(gate_values.dtype),
    )
    places = route_places(group_ids, experts_all, capacity)
    own_places = lax.dynamic_slice_in_dim(
        places, ep_rank * tok_dev * top_count, tok_dev * top_count
    )
    local_slot = places - own_first
    pick_mask = (local_slot[None, :] == slot_range[:, None]).astype(jnp.float32)
    slot_gates = jnp.sum(pick_mask * group_gates.reshape(1, -1), axis=1)
    by_token = pick_mask.reshape(slots_dev, -1, top_count).sum(axis=2).astype(jnp.bfloat16)
    slot_rows = jnp.dot(by_token, group_rows, preferred_element_type=jnp.float32).astype(
        jnp.bfloat16
    )
    stacked_rows = slot_rows.reshape(1, slots_dev, model_width)
    stacked_gates = slot_gates.reshape(1, slots_dev)
    whole_rows, whole_gates = (
        lax.all_gather(stacked_rows, "ctx", axis=0, tiled=True),
        lax.all_gather(stacked_gates.astype(jnp.bfloat16), "ctx", axis=0, tiled=True).astype(
            stacked_gates.dtype
        ),
    )
    row_count = whole_rows.shape[0]
    piece_view = whole_rows.reshape(row_count, exp_dev, capacity, model_width)
    gate_view = whole_gates.reshape(row_count, exp_dev, capacity)
    grad_in = jnp.einsum("necd,efd->necf", piece_view, w_down, preferred_element_type=jnp.float32)
    hid_piece = (gate_view[..., None] * grad_in).astype(jnp.bfloat16)
    gate_piece = jnp.sum(hidden.astype(jnp.float32) * grad_in, axis=3)
    scaled = (gate_view[..., None] * piece_view.astype(jnp.float32)).astype(jnp.bfloat16)
    grad_acc = jnp.einsum("necf,necd->efd", hidden, scaled, preferred_element_type=jnp.float32)
    hid_grad = hid_piece
    partial_value = gate_piece
    grad_acc, hid_grad, partial_value = (grad_acc, hid_grad, partial_value)
    own_terms = summed_on_arrival(partial_value, "ctx", 0)
    score_table = collect(own_terms.reshape(slots_dev), "ep", 0)
    lookup = (
        own_places[:, None] == jnp.arange(score_table.shape[0], dtype=jnp.int32)[None, :]
    ).astype(jnp.float32)
    gate_grad = jnp.sum(lookup * score_table[None, :], axis=1).reshape(tok_dev, top_count)
    return (hid_grad, grad_acc.astype(jnp.bfloat16), gate_grad)


def solution(mesh):
    placed = (
        P(("ctx", "ep"), None),
        P(("ctx", "ep"), None),
        P(("ctx", "ep"), None),
        P(None, "ep", None, "ctx"),
        P("ep", "ctx", None),
    )
    return jax.shard_map(
        per_device,
        mesh=mesh,
        in_specs=placed,
        out_specs=(P(None, "ep", None, "ctx"), P("ep", "ctx", None), P(("ctx", "ep"), None)),
        check_vma=False,
    )
```

profile of v0, /device:TPU:1, one launch (start us, length us, event | category | flops | bytes accessed | tf_op | source)
XLA Modules:
  0.0 270.4 jit_solution(6347631741123845053)
XLA Ops:
  7.2 1.4 broadcast_in_dim.10
  8.6 17.6 %all-to-all-start = ((s32[32,2,8]{2,1,0:T(2,128)}), s32[32,2,8]{2,1,0:T(2,128)S(1)}, u32[]{:S(2)}, u32[]{:S(2)}) async-start(s32[32,2,8]{2,1,0:T(2,128)} %broadcast_in_dim.10), calls=%async_computation | async-start | bytes 65536 | tf_op jit(solution)/shard_map/all_to_all | solution.py:9
  26.2 7.4 %all-to-all-done = s32[32,2,8]{2,1,0:T(2,128)S(1)} async-done(((s32[32,2,8]{2,1,0:T(2,128)}), s32[32,2,8]{2,1,0:T(2,128)S(1)}, u32[]{:S(2)}, u32[]{:S(2)}) %all-to-all-start) | async-done | bytes 2080 | tf_op jit(solution)/shard_map/all_to_all | solution.py:9
  33.6 1.7 broadcast_in_dim.12
  35.3 3.9 %all-to-all-start.2 = ((bf16[32,2,3584]{2,1,0:T(2,128)(2,1)}), bf16[32,2,3584]{2,1,0:T(2,128)(2,1)S(1)}, u32[]{:S(2)}, u32[]{:S(2)}) async-start(bf16[32,2,3584]{2,1,0:T(2,128)(2,1)} %broadcast_in_dim.12), calls=%async_computation.2 | async-start | bytes 917504 | tf_op jit(solution)/shard_map/all_to_all | solution.py:9
  39.5 0.2 fusion.13
  40.0 0.2 fusion.12
  40.4 9.9 %all-to-all-done.2 = bf16[32,2,3584]{2,1,0:T(2,128)(2,1)S(1)} async-done(((bf16[32,2,3584]{2,1,0:T(2,128)(2,1)}), bf16[32,2,3584]{2,1,0:T(2,128)(2,1)S(1)}, u32[]{:S(2)}, u32[]{:S(2)}) %all-to-all-start.2) | async-done | bytes 458784 | tf_op jit(solution)/shard_map/all_to_all | solution.py:9
  50.5 0.9 fusion.5
  51.4 0.7 convert_element_type.66
  52.1 0.6 broadcast_in_dim.11
  52.7 3.6 %all-to-all-start.1 = ((bf16[32,2,8]{2,1,0:T(2,128)(2,1)}), bf16[32,2,8]{2,1,0:T(2,128)(2,1)S(1)}, u32[]{:S(2)}, u32[]{:S(2)}) async-start(bf16[32,2,8]{2,1,0:T(2,128)(2,1)} %broadcast_in_dim.11), calls=%async_computation.1 | async-start | bytes 32768 | tf_op jit(solution)/shard_map/all_to_all | solution.py:9
  56.3 1.3 dynamic-slice
  58.3 4.9 %all-to-all-done.1 = bf16[32,2,8]{2,1,0:T(2,128)(2,1)S(1)} async-done(((bf16[32,2,8]{2,1,0:T(2,128)(2,1)}), bf16[32,2,8]{2,1,0:T(2,128)(2,1)S(1)}, u32[]{:S(2)}, u32[]{:S(2)}) %all-to-all-start.1) | async-done | bytes 1056 | tf_op jit(solution)/shard_map/all_to_all | solution.py:9
  63.4 0.2 dynamic-update-slice
  63.6 50.1 %all-reduce = bf16[896]{0:T(1024)(128)(2,1)S(1)} all-reduce(bf16[896]{0:T(1024)(128)(2,1)S(1)} %dynamic-update-slice), channel_id=2, replica_groups=mesh['ctx'=32,'ep'=32] {'ctx'}, use_global_device_ids=true, to_apply=%add | all-reduce | flops 896 | bytes 3584
  113.7 0.3 reshape.103
  114.1 62.7 %all-gather.5.cloned.1.call-done = bf16[32,28,3584]{2,1,0:T(8,128)(2,1)} async-done(((bf16[1,28,3584]{2,1,0:T(8,128)(2,1)}), bf16[32,28,3584]{2,1,0:T(8,128)(2,1)}) %all-gather.5.cloned.1.call-update) | async-done | bytes 6422544 | tf_op jit(solution)/shard_map/all_gather | solution.py:75
  176.8 6.6 %copy.34 = bf16[32,28,3584]{2,0,1:T(8,128)(2,1)S(1)} copy(bf16[32,28,3584]{2,1,0:T(8,128)(2,1)} %all-gather.5.cloned.1.call-done) | data formatting | bytes 12845056 | tf_op jit(solution)/shard_map/all_gather | solution.py:75
  183.4 2.7 copy-done.1
  186.1 1.9 multiply_reduce_fusion
  188.0 0.7 copy.38
  188.7 13.4 %all-to-all-start.3 = ((f32[32,1,4,7]{3,2,1,0:T(4,128)}), f32[32,1,4,7]{3,2,1,0:T(4,128)S(1)}, u32[]{:S(2)}, u32[]{:S(2)}) async-start(f32[32,1,4,7]{3,2,1,0:T(4,128)} %copy.38), calls=%async_computation.3 | async-start | bytes 131072 | tf_op jit(solution)/shard_map/all_to_all | solution.py:32
  202.2 23.3 %all-to-all-done.3 = f32[32,1,4,7]{3,2,1,0:T(4,128)S(1)} async-done(((f32[32,1,4,7]{3,2,1,0:T(4,128)}), f32[32,1,4,7]{3,2,1,0:T(4,128)S(1)}, u32[]{:S(2)}, u32[]{:S(2)}) %all-to-all-start.3) | async-done | bytes 3616 | tf_op jit(solution)/shard_map/all_to_all | solution.py:32
  225.6 0.6 broadcast_in_dim.14
  226.2 28.2 %all-to-all-start.4 = ((f32[32,1,28]{2,1,0:T(1,128)}), f32[32,1,28]{2,1,0:T(1,128)S(1)}, u32[]{:S(2)}, u32[]{:S(2)}) async-start(f32[32,1,28]{2,1,0:T(1,128)} %broadcast_in_dim.14), calls=%async_computation.4 | async-start | bytes 32768 | tf_op jit(solution)/shard_map/all_to_all | solution.py:9
  254.4 5.5 %fusion.4 = bf16[4,48,3584]{2,1,0:T(8,128)(2,1)} fusion(bf16[32,4,7,3584]{3,0,2,1:T(8,128)(2,1)} %bitcast.43, f32[32,4,7]{0,2,1:T(8,128)S(1)} %copy.32, bf16[32,4,7,48]{3,1,2,0:T(4,128)(2,1)S(1)} %copy-done.2), kind=kOutput, calls=%fused_computation.5 | convolution fusion | flops 318603264 | bytes 7888384 | tf_op jit(solution)/shard_map/necf,necd->efd/dot_general | solution.py:87
  259.9 0.8 copy.39
  260.7 0.7 all-to-all-done.4
  261.4 0.5 broadcast.56
  261.9 0.7 reduce.4
  262.9 0.6 reshape.101
  (32 shorter events, 1.7 us)
Async XLA Ops:
  7.2 178.9 %copy-start = (bf16[4,48,3584]{2,1,0:T(8,128)(2,1)S(1)}, bf16[4,48,3584]{2,1,0:T(8,128)(2,1)}, u32[]{:S(2)}) copy-start(bf16[4,48,3584]{2,1,0:T(8,128)(2,1)} %param.9) | copy-start | bytes 4128772
  8.6 25.0 %all-to-all-start = ((s32[32,2,8]{2,1,0:T(2,128)}), s32[32,2,8]{2,1,0:T(2,128)S(1)}, u32[]{:S(2)}, u32[]{:S(2)}) async-start(s32[32,2,8]{2,1,0:T(2,128)} %broadcast_in_dim.10), calls=%async_computation | async-start | bytes 65536 | tf_op jit(solution)/shard_map/all_to_all | solution.py:9
  35.3 15.0 %all-to-all-start.2 = ((bf16[32,2,3584]{2,1,0:T(2,128)(2,1)}), bf16[32,2,3584]{2,1,0:T(2,128)(2,1)S(1)}, u32[]{:S(2)}, u32[]{:S(2)}) async-start(bf16[32,2,3584]{2,1,0:T(2,128)(2,1)} %broadcast_in_dim.12), calls=%async_computation.2 | async-start | bytes 917504 | tf_op jit(solution)/shard_map/all_to_all | solution.py:9
  39.3 137.5 %all-gather.5.cloned.1.call-start = ((), (), s32[]{:S(2)}) async-start(), calls=%async_computation.5 | async-start | bytes 7569408 | tf_op jit(solution)/shard_map/all_gather | solution.py:75
  52.7 10.4 %all-to-all-start.1 = ((bf16[32,2,8]{2,1,0:T(2,128)(2,1)}), bf16[32,2,8]{2,1,0:T(2,128)(2,1)S(1)}, u32[]{:S(2)}, u32[]{:S(2)}) async-start(bf16[32,2,8]{2,1,0:T(2,128)(2,1)} %broadcast_in_dim.11), calls=%async_computation.1 | async-start | bytes 32768 | tf_op jit(solution)/shard_map/all_to_all | solution.py:9
  114.1 72.0 %copy-start.2 = (bf16[32,4,7,48]{3,1,2,0:T(4,128)(2,1)S(1)}, bf16[32,4,7,48]{3,1,2,0:T(4,128)(2,1)}, u32[]{:S(2)}) copy-start(bf16[32,4,7,48]{3,1,2,0:T(4,128)(2,1)} %param.8) | copy-start | bytes 258052
  183.4 2.7 copy-start.1
  188.7 36.7 %all-to-all-start.3 = ((f32[32,1,4,7]{3,2,1,0:T(4,128)}), f32[32,1,4,7]{3,2,1,0:T(4,128)S(1)}, u32[]{:S(2)}, u32[]{:S(2)}) async-start(f32[32,1,4,7]{3,2,1,0:T(4,128)} %copy.38), calls=%async_computation.3 | async-start | bytes 131072 | tf_op jit(solution)/shard_map/all_to_all | solution.py:32
  226.2 35.2 %all-to-all-start.4 = ((f32[32,1,28]{2,1,0:T(1,128)}), f32[32,1,28]{2,1,0:T(1,128)S(1)}, u32[]{:S(2)}, u32[]{:S(2)}) async-start(f32[32,1,28]{2,1,0:T(1,128)} %broadcast_in_dim.14), calls=%async_computation.4 | async-start | bytes 32768 | tf_op jit(solution)/shard_map/all_to_all | solution.py:9
Sparse Core Ops, SparseCore 0:
  51.5 125.1 all-gather.4
where the time goes:
time: 271 us; the launch traced here: 270 us
  waiting for transfers between devices  109 us (40%)
  starting transfers between devices  66.8 us (25%)
  blocking collectives  50.1 us (18%)
  local copies, waits for them, and re-layouts  19.2 us (7%)
  between operations  14.9 us (5%)
  matrix products  8.28 us (3%)
    all_gather x1, waiting for transfers between devices, per_device(): lax.all_gather(stacked_rows, 'ctx', axis=0, tiled=True)  62.7 us
    all_to_all x4, starting transfers between devices, from_everyone(): lax.all_to_all(jnp.broadcast_to(value[None], (count, *value.shape)), axis...  53.4 us
    unnamed x1, blocking collectives  50.1 us
    all_to_all x1, waiting for transfers between devices, summed_on_arrival(): lax.all_to_all(cut_along(value, dim, count), axis, 0, 0, tiled=True)  23.3 us
    all_to_all x4, waiting for transfers between devices, from_everyone(): lax.all_to_all(jnp.broadcast_to(value[None], (count, *value.shape)), axis...  22.8 us
    all_to_all x1, starting transfers between devices, summed_on_arrival(): lax.all_to_all(cut_along(value, dim, count), axis, 0, 0, tiled=True)  13.4 us
    all_gather x1, local copies, waits for them, and re-layouts, per_device(): lax.all_gather(stacked_rows, 'ctx', axis=0, tiled=True)  6.6 us
    dot_general x1, matrix products, per_device(): jnp.einsum('necf,necd->efd', hidden, scaled, preferred_element_type=jnp.f...  5.5 us
  transfers between devices with their start and end apart: 6, of which 6 were waited for; matrix products, arithmetic and copies ran while one was open for 4% of the time, Pallas kernels for 0%

commit v1 on v0

v1 whole, which is shorter than its diff:
```python
import functools

import jax
import jax.numpy as jnp
from jax import lax
from jax.experimental import pallas as pl
from jax.experimental.pallas import tpu as pltpu
from jax.sharding import PartitionSpec as P

MESH = pl.DeviceIdType.MESH
F32, BF16 = jnp.float32, jnp.bfloat16

NZ = 32
NE = 32
CHUNKS, PER = 8, 4
LANES = 3584 + 128
COLOURS = (
    ((0, 1920), (0, 1024), (1024, 896)),
    ((1920, 1792), (1920, 896), (2816, 896)),
)


def kernel(
    own_ref, hid_ref, w_ref,
    hg_ref, dw_ref, val_ref,
    zbuf, xall, dwacc, msg, rbuf, fbuf,
    zs_sem, zr_sem, s_sem, r_sem, d_sem, ms_sem, mr_sem, fs_sem, fr_sem,
):
    z, ep = lax.axis_index("ctx"), lax.axis_index("ep")
    core, px, py = ep % 2, ep // 8, (ep // 2) % 4
    experts, capacity = 4, hid_ref.shape[1]
    width = w_ref.shape[0]
    part = width // experts
    model = w_ref.shape[1]

    def along_z(d):
        return ((z + d + NZ) % NZ, ep)

    def chip(x, y):
        return ((x + 4) % 4 * 4 + (y + 4) % 4) * 2 + core

    def at(colour, dp, dq):
        return chip(px + dq, py + dp) if colour == 0 else chip(px + dp, py + dq)

    partner = (z, ep + 1 - 2 * core)

    barrier = pltpu.get_barrier_semaphore()
    near = [along_z(d) for d in (1, 2, 3, 4, -1, -2, -3, -4)]
    near += [(z, at(0, 1, 0)), (z, at(0, -1, 0)), (z, at(0, 0, 1)), (z, at(0, 0, -1)), partner]
    for peer in near:
        pl.semaphore_signal(barrier, inc=1, device_id=peer, device_id_type=MESH)
    pl.semaphore_wait(barrier, len(near))

    def z_send(src, slot, d):
        pltpu.make_async_remote_copy(
            src_ref=src, dst_ref=zbuf.at[slot], send_sem=zs_sem.at[0], recv_sem=zr_sem.at[slot],
            device_id=along_z(d), device_id_type=MESH,
        ).start()

    for j in (4, 3, 2, 1):
        z_send(own_ref, j - 1, j)
        z_send(own_ref, 16 + j, -j)
    zbuf[16] = own_ref[...]
    dwacc[...] = jnp.zeros_like(dwacc)

    def z_wait(slot):
        pltpu.make_async_copy(own_ref, zbuf.at[slot], zr_sem.at[slot]).wait()

    def chunk_of(n):
        up = 1 - n % 2
        return 4 * up + n // 2, up, n // 2

    def group_of(n, i):
        _, up, w = chunk_of(n)
        return (z + 2 * NZ + up * (4 * w + i) - (1 - up) * (4 * w + i + 1)) % NZ

    def fetch(n):
        c, up, w = chunk_of(n)

        @pl.when(up == 1)
        def _():
            @pl.when(w > 0)
            def _():
                z_wait(16 + 4 * w)
                for j in (4, 3, 2, 1):
                    if j < 4:
                        z_send(zbuf.at[16 + 4 * w], 16 + 4 * w + j, -j)
                    else:
                        @pl.when(w < 3)
                        def _():
                            z_send(zbuf.at[16 + 4 * w], 16 + 4 * w + 4, -4)
            for i in (1, 2, 3):
                z_wait(16 + 4 * w + i)

        @pl.when(up == 0)
        def _():
            z_wait(4 * w + 3)

            @pl.when(w < 3)
            def _():
                for j in (4, 3, 2, 1):
                    z_send(zbuf.at[4 * w + 3], 4 * w + 3 + j, j)
            for i in (0, 1, 2):
                z_wait(4 * w + i)

        rows = [zbuf[4 * c + i].astype(F32) for i in range(PER)]
        xall[c, ep] = jnp.concatenate(rows, axis=0).astype(BF16)

    def block(c, e, lanes):
        return xall.at[c, e, :, pl.ds(*lanes)]

    def send(c, e, lanes, to, sem):
        pltpu.make_async_remote_copy(
            src_ref=block(c, e, lanes), dst_ref=block(c, e, lanes), send_sem=s_sem.at[c], recv_sem=sem,
            device_id=to, device_id_type=MESH,
        ).start()

    def share(c, colour, dp, dq):
        send(c, at(colour, dp, dq), COLOURS[colour][0], partner, d_sem.at[c])

    def send_p(c, colour, dp, dq, step, piece):
        send(c, at(colour, dp, dq), COLOURS[colour][piece], (z, at(colour, step, 0)),
             r_sem.at[c, colour, (dp - step) % 4 * 4 + dq % 4])

    def send_q(c, colour, dp, dq, step, piece):
        send(c, at(colour, dp, dq), COLOURS[colour][piece], (z, at(colour, 0, step)),
             r_sem.at[c, colour, dp % 4 * 4 + (dq - step) % 4])

    def wait(c, colour, dp, dq):
        ref = block(c, at(colour, dp, dq), COLOURS[colour][0])
        pltpu.make_async_copy(ref, ref, r_sem.at[c, colour, dp % 4 * 4 + dq % 4]).wait()

    def stage1(c):
        for colour in (0, 1):
            send_p(c, colour, 0, 0, 1, 0)
            send_p(c, colour, 0, 0, -1, 0)
        for colour in (0, 1):
            share(c, colour, 0, 0)

    def stage2(c):
        for colour in (0, 1):
            for dp in (-1, 1):
                wait(c, colour, dp, 0)
                send_p(c, colour, dp, 0, -dp, 1 if dp < 0 else 2)
        for colour in (0, 1):
            for dp in (0, -1, 1):
                send_q(c, colour, dp, 0, 1, 0)
                send_q(c, colour, dp, 0, -1, 0)
        for colour in (0, 1):
            for dp in (-1, 1):
                share(c, colour, dp, 0)

    def stage3(c):
        for colour in (0, 1):
            wait(c, colour, 2, 0)
            send_q(c, colour, 2, 0, 1, 0)
            send_q(c, colour, 2, 0, -1, 0)
        for dp in (0, -1, 1):
            for colour in (0, 1):
                for dq in (-1, 1):
                    wait(c, colour, dp, dq)
                    send_q(c, colour, dp, dq, -dq, 1 if dq < 0 else 2)
        for colour in (0, 1):
            share(c, colour, 2, 0)
            for dp in (0, -1, 1):
                for dq in (-1, 1):
                    share(c, colour, dp, dq)

    def stage4(c):
        for colour in (0, 1):
            for dq in (-1, 1):
                wait(c, colour, 2, dq)
                send_q(c, colour, 2, dq, -dq, 1 if dq < 0 else 2)
        for colour in (0, 1):
            for dp in (0, -1, 1):
                wait(c, colour, dp, 2)
                share(c, colour, dp, 2)
            for dq in (-1, 1):
                share(c, colour, 2, dq)

    def stage5(c):
        for colour in (0, 1):
            wait(c, colour, 2, 2)
            share(c, colour, 2, 2)

    rows256 = NE * 2 * PER

    def compute(n):
        c, _, _ = chunk_of(n)
        half = xall.at[c, pl.ds(0, NE // 2)]
        pltpu.make_async_copy(half, half, d_sem.at[c]).wait()
        gates = xall[c, :, :, pl.ds(model, 128)].reshape(rows256, 128)
        e_at = lax.broadcasted_iota(jnp.int32, (128, width), 0)
        f_at = lax.broadcasted_iota(jnp.int32, (128, width), 1)
        pick = jnp.where(e_at == experts * ep + f_at // part, 1.0, 0.0).astype(BF16)
        gate = jnp.dot(gates, pick, preferred_element_type=F32)
        live = gate > 0
        r_at = lax.broadcasted_iota(jnp.int32, (rows256, rows256), 0)
        c_at = lax.broadcasted_iota(jnp.int32, (rows256, rows256), 1)
        earlier = ((r_at % 8) // 2 == (c_at % 8) // 2) & (c_at < r_at)
        slot = jnp.dot(
            jnp.where(earlier, 1.0, 0.0).astype(BF16), jnp.where(live, 1.0, 0.0).astype(BF16),
            preferred_element_type=F32,
        )
        slot = jnp.where(live, slot, -1.0).reshape(NE, 8, width)
        rows = xall[c, :, :, pl.ds(0, model)].reshape(rows256, model)
        grad_in = lax.dot_general(rows, w_ref[...], (((1,), (1,)), ((), ())), preferred_element_type=F32)
        own_group = [hid_ref[group_of(n, i)].astype(F32) for i in range(PER)]
        row8 = lax.broadcasted_iota(jnp.int32, (8, width), 0) // 2
        hid = jnp.zeros((NE, 8, width), F32)
        for s in range(capacity):
            wide = jnp.zeros((8, width), F32)
            for i in range(PER):
                wide = jnp.where(row8 == i, own_group[i][s : s + 1, :], wide)
            hid = jnp.where(slot == float(s), wide[None], hid)
        grad3 = grad_in.reshape(NE, 8, width)
        gate3 = gate.reshape(NE, 8, width)
        out = (gate3 * grad3).astype(BF16).astype(F32)
        term = hid * grad3
        terms = []
        outs = []
        for s in range(capacity):
            here = slot == float(s)
            o = jnp.sum(jnp.where(here, out, 0.0), axis=0)
            t = jnp.sum(jnp.where(here, term, 0.0), axis=0)
            outs.append(o + pltpu.roll(o, 7, 0))
            terms.append(t + pltpu.roll(t, 7, 0))
        for i in range(PER):
            hg_ref[group_of(n, i)] = jnp.concatenate([o[2 * i : 2 * i + 1] for o in outs], axis=0)
        t = jnp.concatenate(terms, axis=0)
        hi = t.astype(BF16)
        rest = t - hi.astype(F32)
        mid = rest.astype(BF16)
        low = (rest - mid.astype(F32)).astype(BF16)
        k_at = lax.broadcasted_iota(jnp.int32, (width, 128), 0)
        l_at = lax.broadcasted_iota(jnp.int32, (width, 128), 1)
        fold = jnp.where(k_at // part == l_at, 1.0, 0.0).astype(BF16)
        sums = sum(jnp.dot(p, fold, preferred_element_type=F32) for p in (hi, mid, low))
        lanes = sums[0:8]
        for s in range(1, capacity):
            lanes = lanes + pltpu.roll(sums[8 * s : 8 * s + 8], experts * s, 1)
        for i in range(PER):
            msg[4 * c + i] = lanes[2 * i : 2 * i + 1]
        weighted = (gate3 * hid).reshape(rows256, width).T.astype(BF16)
        step = 512
        for m in range(model // step):
            cols = pl.ds(m * step, step)
            piece = xall[c, :, :, cols].reshape(rows256, step)
            dwacc[:, cols] += jnp.dot(weighted, piece, preferred_element_type=F32)
        for i in range(PER):
            def put(i=i):
                pltpu.make_async_remote_copy(
                    src_ref=msg.at[4 * c + i], dst_ref=rbuf.at[4 * c + i],
                    send_sem=ms_sem.at[0], recv_sem=mr_sem.at[0],
                    device_id=(group_of(n, i), ep), device_id_type=MESH,
                ).start()
            if i == 0:
                pl.when(n > 0)(put)

                @pl.when(n == 0)
                def _():
                    rbuf[16] = msg[16]
            else:
                put()

    fetch(0)

    def step(n, carry):
        for back, stage in enumerate((stage1, stage2, stage3, stage4, stage5)):
            @pl.when((n >= back) & (n < CHUNKS + back))
            def _(back=back, stage=stage):
                stage(chunk_of(n - back)[0])

        @pl.when(n < CHUNKS - 1)
        def _():
            fetch(n + 1)

        @pl.when(n >= 5)
        def _():
            compute(n - 5)
        return carry

    lax.fori_loop(0, CHUNKS + 5, step, 0)
    dw_ref[...] = dwacc[...].astype(BF16)

    mine = xall[4, :, :, pl.ds(model, 128)].astype(F32).reshape(rows256, 128) > 0
    at_row = lax.broadcasted_iota(jnp.int32, (rows256, 128), 0)
    counts = []
    for r in range(2):
        before = mine & (at_row % 8 < 2) & (at_row < ep * 8 + r)
        counts.append(jnp.sum(jnp.where(before, 1.0, 0.0), axis=0, keepdims=True))

    most = rbuf.at[pl.ds(0, NZ - 1)]
    pltpu.make_async_copy(most, most, mr_sem.at[0]).wait()
    total = jnp.sum(rbuf[...], axis=0)
    s_at = lax.broadcasted_iota(jnp.int32, (8, 128), 0)
    l_at = lax.broadcasted_iota(jnp.int32, (8, 128), 1)
    spread = jnp.where(l_at // experts == s_at, total, 0.0)
    a_at = lax.broadcasted_iota(jnp.int32, (128, 128), 0)
    b_at = lax.broadcasted_iota(jnp.int32, (128, 128), 1)
    place = jnp.where(b_at == experts * ep + a_at % experts, 1.0, 0.0)
    fbuf[ep] = jnp.dot(spread, place, preferred_element_type=F32, precision=lax.Precision.HIGHEST)

    def tell(d, carry):
        pltpu.make_async_remote_copy(
            src_ref=fbuf.at[ep], dst_ref=fbuf.at[ep], send_sem=fs_sem.at[0], recv_sem=fr_sem.at[0],
            device_id=(z, (ep + d) % NE), device_id_type=MESH,
        ).start()
        return carry

    lax.fori_loop(1, NE, tell, 0)
    most = fbuf.at[pl.ds(0, NE - 1)]
    pltpu.make_async_copy(most, most, fr_sem.at[0]).wait()
    table = jnp.sum(fbuf[...], axis=0)
    vals = []
    for r in range(2):
        v = jnp.zeros((1, 128), F32)
        for s in range(capacity):
            v = jnp.where(counts[r] == float(s), table[s : s + 1], v)
        vals.append(v)
    val_ref[...] = jnp.concatenate(vals, axis=0)

    sent = zbuf.at[pl.ds(0, NZ - 1)]
    pltpu.make_async_copy(sent, sent, zs_sem.at[0]).wait()
    for c in range(CHUNKS):
        sent = xall.at[c, pl.ds(0, NE - 1)]
        pltpu.make_async_copy(sent, sent, s_sem.at[c]).wait()
    sent = msg.at[pl.ds(0, NZ - 1)]
    pltpu.make_async_copy(sent, sent, ms_sem.at[0]).wait()
    sent = fbuf.at[pl.ds(0, NE - 1)]
    pltpu.make_async_copy(sent, sent, fs_sem.at[0]).wait()


def per_device(out_grad, expert_ids, gate_values, hidden, w_down):
    groups, experts, capacity, part = hidden.shape
    model = out_grad.shape[1]
    width = experts * part
    named = expert_ids[:, :, None] == jnp.arange(128, dtype=jnp.int32)[None, None, :]
    gates = jnp.sum(jnp.where(named, gate_values[:, :, None], 0.0), axis=1)
    own = jnp.concatenate([out_grad, gates.astype(BF16)], axis=1)
    hid = jnp.transpose(hidden, (0, 2, 1, 3)).reshape(groups, capacity, width)
    vmem = pl.BlockSpec(memory_space=pltpu.VMEM)
    hid_grad, weight_grad, values = pl.pallas_call(
        kernel,
        out_shape=(
            jax.ShapeDtypeStruct((groups, capacity, width), F32),
            jax.ShapeDtypeStruct((width, model), BF16),
            jax.ShapeDtypeStruct((2, 128), F32),
        ),
        in_specs=[vmem] * 3,
        out_specs=(vmem,) * 3,
        scratch_shapes=[
            pltpu.VMEM((NZ, 2, LANES), BF16),
            pltpu.VMEM((CHUNKS, NE, 8, LANES), BF16),
            pltpu.VMEM((width, model), F32),
            pltpu.VMEM((NZ, 1, 128), F32),
            pltpu.VMEM((NZ, 1, 128), F32),
            pltpu.VMEM((NE, 8, 128), F32),
            pltpu.SemaphoreType.DMA((1,)),
            pltpu.SemaphoreType.DMA((NZ,)),
            pltpu.SemaphoreType.DMA((CHUNKS,)),
            pltpu.SemaphoreType.DMA((CHUNKS, 2, 16)),
            pltpu.SemaphoreType.DMA((CHUNKS,)),
            pltpu.SemaphoreType.DMA((1,)),
            pltpu.SemaphoreType.DMA((1,)),
            pltpu.SemaphoreType.DMA((1,)),
            pltpu.SemaphoreType.DMA((1,)),
        ],
        compiler_params=pltpu.CompilerParams(
            collective_id=0, has_side_effects=True, vmem_limit_bytes=56 * 1024 * 1024
        ),
    )(own, hid, w_down.reshape(width, model))
    hid_grad = hid_grad.astype(BF16).reshape(groups, capacity, experts, part)
    picked = jnp.where(named, values[:, None, :], 0.0)
    return (
        jnp.transpose(hid_grad, (0, 2, 1, 3)),
        weight_grad.reshape(experts, part, model),
        jnp.sum(picked, axis=2),
    )


def solution(mesh):
    placed = (
        P(("ctx", "ep"), None),
        P(("ctx", "ep"), None),
        P(("ctx", "ep"), None),
        P(None, "ep", None, "ctx"),
        P("ep", "ctx", None),
    )
    return jax.shard_map(
        per_device,
        mesh=mesh,
        in_specs=placed,
        out_specs=(P(None, "ep", None, "ctx"), P("ep", "ctx", None), P(("ctx", "ep"), None)),
        check_vma=False,
    )
```

time: 271 us -> 117 us (0.43)
  waiting for transfers between devices: 109 us -> 0 us
  Pallas kernels: 0 us -> 108 us
  starting transfers between devices: 66.8 us -> 0 us
  blocking collectives: 50.1 us -> 0 us
  local copies, waits for them, and re-layouts: 19.2 us -> 3.83 us
  between operations: 14.9 us -> 0.68 us
  matrix products: 8.28 us -> 0 us
    pallas_call x0 -> x1, Pallas kernels: none -> 108 us  [per_device(): pl.pallas_call(kernel, out_shape=(jax.ShapeDtypeStruct((groups, capacity,...]
    all_to_all x5 -> x0, starting transfers between devices: 66.8 us -> none  [the longest x4 53.4 us: from_everyone(): lax.all_to_all(jnp.broadcast_to(value[None], (count, *value.shape)), axis...]
    all_gather x1 -> x0, waiting for transfers between devices: 62.7 us -> none  [per_device(): lax.all_gather(stacked_rows, 'ctx', axis=0, tiled=True)]
    unnamed x1 -> x0, blocking collectives: 50.1 us -> none
    all_to_all x5 -> x0, waiting for transfers between devices: 46.1 us -> none  [the longest x1 23.3 us: summed_on_arrival(): lax.all_to_all(cut_along(value, dim, count), axis, 0, 0, tiled=True)]
    dot_general x3 -> x0, matrix products: 8.28 us -> none  [the longest x1 5.5 us: per_device(): jnp.einsum('necf,necd->efd', hidden, scaled, preferred_element_type=jnp.f...]
    all_gather x1 -> x0, local copies, waits for them, and re-layouts: 6.6 us -> none  [per_device(): lax.all_gather(stacked_rows, 'ctx', axis=0, tiled=True)]
    broadcast_in_dim x5 -> x0, local copies, waits for them, and re-layouts: 4.44 us -> none  [from_everyone(): jnp.broadcast_to(value[None], (count, *value.shape))]
  transfers between devices with their start and end apart: 6 -> 0, of which waited for: 6 -> 0; matrix products, arithmetic and copies ran while one was open for 4% -> 0% of each run, Pallas kernels for 0% -> 0%
where the time goes in v1:
time: 117 us
  Pallas kernels  108 us (92%)
  other arithmetic  4.62 us (4%)
  local copies, waits for them, and re-layouts  3.83 us (3%)
    pallas_call x1, Pallas kernels, per_device(): pl.pallas_call(kernel, out_shape=(jax.ShapeDtypeStruct((groups, capacity,...  108 us

profile of v1, /device:TPU:1, one launch (start us, length us, event | category | flops | bytes accessed | tf_op | source)
XLA Modules:
  0.0 117.0 jit_solution(4606298640068658429)
XLA Ops:
  0.6 0.0 copy-start.1
  0.6 0.8 select_reduce_fusion.1
  1.5 1.3 %pad_maximum_fusion.own_ref = bf16[2,3712]{1,0:T(2,128)(2,1)} fusion(bf16[2,128]{1,0:T(2,128)(2,1)S(1)} %select_reduce_fusion.1, bf16[2,3584]{1,0:T(2,128)(2,1)} %param.5), kind=kLoop, calls=%fused_computation | loop fusion | flops 29696 | bytes 29696 | tf_op jit(solution)/shard_map/concatenate | solution.py:340
  2.8 1.8 %reshape.25.hid_ref = bf16[32,7,192]{2,1,0:T(8,128)(2,1)} reshape(bf16[32,7,4,48]{3,2,1,0:T(4,128)(2,1)} %bitcast.9) | data formatting | bytes 172032 | tf_op jit(solution)/shard_map/reshape | solution.py:341
  4.6 107.9 %shard_map.76 = (f32[32,7,192]{2,1,0:T(8,128)}, bf16[192,3584]{1,0:T(8,128)(2,1)}, f32[2,128]{1,0:T(2,128)}) custom-call(bf16[2,3712]{1,0:T(2,128)(2,1)} %pad_maximum_fusion.own_ref, bf16[32,7,192]{2,1,0:T(8,128)(2,1)} %reshape.25.hid_ref, bf16[192,3584]{1,0:T(8,128)(2,1)} %bitcast.6), custom_call_target="tpu_custom_call" | custom-call | tf_op jit(solution)/shard_map/pallas_call | solution.py:343
  112.5 0.0 copy-start
  112.5 1.1 convert_element_type.7
  113.6 0.0 copy-done.1
  113.6 1.4 %select_reduce_fusion = f32[2,8]{1,0:T(2,128)} fusion(f32[2,128]{1,0:T(2,128)} %get-tuple-element.8, s32[2,8]{1,0:T(2,128)S(1)} %copy-done.1), kind=kLoop, calls=%fused_computation.1 | loop fusion | flops 6128 | bytes 1152 | tf_op jit(solution)/shard_map/reduce_sum | solution.py:378
  115.0 0.2 reshape.23
  115.1 0.8 copy.15
  115.9 0.0 copy-done
  115.9 1.1 copy.18
  (1 shorter events, 0.0 us)
Async XLA Ops:
  0.6 113.0 %copy-start.1 = (s32[2,8]{1,0:T(2,128)S(1)}, s32[2,8]{1,0:T(2,128)}, u32[]{:S(2)}) copy-start(s32[2,8]{1,0:T(2,128)} %param.6) | copy-start | bytes 196
  112.5 3.5 %copy-start = (bf16[192,3584]{1,0:T(8,128)(2,1)S(1)}, bf16[192,3584]{1,0:T(8,128)(2,1)}, u32[]{:S(2)}) copy-start(bf16[192,3584]{1,0:T(8,128)(2,1)} %get-tuple-element.7) | copy-start | bytes 4128772

commit v2 on v1

--- a/solution.py
+++ b/solution.py
@@ -1,5 +1,3 @@
-import functools
-
 import jax
 import jax.numpy as jnp
 from jax import lax
@@ -20,18 +18,31 @@
 )
 
 
+ORDER = (4, 0, 5, 6, 2, 7, 3, 1)
+
+
 def kernel(
-    own_ref, hid_ref, w_ref,
-    hg_ref, dw_ref, val_ref,
+    rows_hbm, ids_hbm, gates_hbm, hid_hbm, w_hbm,
+    hg_ref, dw_ref, gg_ref,
     zbuf, xall, dwacc, msg, rbuf, fbuf,
-    zs_sem, zr_sem, s_sem, r_sem, d_sem, ms_sem, mr_sem, fs_sem, fr_sem,
+    ids_ref, gates_ref, hid_ref, w_ref, pick_ref, earlier_ref,
+    zs_sem, zr_sem, s_sem, r_sem, d_sem, ms_sem, mr_sem, fs_sem, fr_sem, io_sem,
 ):
+    model = rows_hbm.shape[1]
+    loads = [
+        pltpu.make_async_copy(src, dst, io_sem.at[i])
+        for i, (src, dst) in enumerate((
+            (rows_hbm, zbuf.at[16, :, pl.ds(0, model)]), (ids_hbm, ids_ref), (gates_hbm, gates_ref),
+            (hid_hbm, hid_ref), (w_hbm, w_ref),
+        ))
+    ]
+    for load in loads:
+        load.start()
     z, ep = lax.axis_index("ctx"), lax.axis_index("ep")
     core, px, py = ep % 2, ep // 8, (ep // 2) % 4
     experts, capacity = 4, hid_ref.shape[1]
     width = w_ref.shape[0]
     part = width // experts
-    model = w_ref.shape[1]
 
     def along_z(d):
         return ((z + d + NZ) % NZ, ep)
@@ -49,6 +60,15 @@
     near += [(z, at(0, 1, 0)), (z, at(0, -1, 0)), (z, at(0, 0, 1)), (z, at(0, 0, -1)), partner]
     for peer in near:
         pl.semaphore_signal(barrier, inc=1, device_id=peer, device_id_type=MESH)
+    for load in loads[:3]:
+        load.wait()
+    ids = ids_ref[...]
+    e_lane = lax.broadcasted_iota(jnp.int32, (2, 128), 1)
+    spread = jnp.zeros((2, 128), F32)
+    for k in range(ids.shape[1]):
+        spread = jnp.where(e_lane == ids[:, k : k + 1], gates_ref[:, k : k + 1], spread)
+    zbuf[16, :, pl.ds(model, 128)] = spread.astype(BF16)
+
     pl.semaphore_wait(barrier, len(near))
 
     def z_send(src, slot, d):
@@ -57,52 +77,50 @@
             device_id=along_z(d), device_id_type=MESH,
         ).start()
 
+    own = zbuf.at[16]
     for j in (4, 3, 2, 1):
-        z_send(own_ref, j - 1, j)
-        z_send(own_ref, 16 + j, -j)
-    zbuf[16] = own_ref[...]
+        z_send(own, j - 1, j)
+        z_send(own, 16 + j, -j)
     dwacc[...] = jnp.zeros_like(dwacc)
+    rows256 = NE * 2 * PER
+    e_at = lax.broadcasted_iota(jnp.int32, (128, width), 0)
+    f_at = lax.broadcasted_iota(jnp.int32, (128, width), 1)
+    pick_ref[...] = jnp.where(e_at == experts * ep + f_at // part, 1.0, 0.0).astype(BF16)
+    r_at = lax.broadcasted_iota(jnp.int32, (rows256, rows256), 0)
+    c_at = lax.broadcasted_iota(jnp.int32, (rows256, rows256), 1)
+    earlier = ((r_at % 8) // 2 == (c_at % 8) // 2) & (c_at < r_at)
+    earlier_ref[...] = jnp.where(earlier, 1.0, 0.0).astype(BF16)
 
     def z_wait(slot):
-        pltpu.make_async_copy(own_ref, zbuf.at[slot], zr_sem.at[slot]).wait()
+        pltpu.make_async_copy(own, zbuf.at[slot], zr_sem.at[slot]).wait()
 
     def chunk_of(n):
-        up = 1 - n % 2
-        return 4 * up + n // 2, up, n // 2
-
-    def group_of(n, i):
-        _, up, w = chunk_of(n)
+        c = 0
+        for i, one in enumerate(ORDER):
+            c = c + jnp.where(n == i, one, 0)
+        return c
+
+    def group_of(c, i):
+        up, w = c // 4, c % 4
         return (z + 2 * NZ + up * (4 * w + i) - (1 - up) * (4 * w + i + 1)) % NZ
 
+    def forward(w):
+        low, high = 4 * w + 3, 20 + 4 * w
+        z_wait(low)
+        z_wait(high)
+        for j in (4, 3, 2, 1):
+            z_send(zbuf.at[low], low + j, j)
+            if high + j < 32:
+                z_send(zbuf.at[high], high + j, -j)
+
     def fetch(n):
-        c, up, w = chunk_of(n)
-
-        @pl.when(up == 1)
-        def _():
-            @pl.when(w > 0)
-            def _():
-                z_wait(16 + 4 * w)
-                for j in (4, 3, 2, 1):
-                    if j < 4:
-                        z_send(zbuf.at[16 + 4 * w], 16 + 4 * w + j, -j)
-                    else:
-                        @pl.when(w < 3)
-                        def _():
-                            z_send(zbuf.at[16 + 4 * w], 16 + 4 * w + 4, -4)
-            for i in (1, 2, 3):
-                z_wait(16 + 4 * w + i)
-
-        @pl.when(up == 0)
-        def _():
-            z_wait(4 * w + 3)
-
-            @pl.when(w < 3)
-            def _():
-                for j in (4, 3, 2, 1):
-                    z_send(zbuf.at[4 * w + 3], 4 * w + 3 + j, j)
-            for i in (0, 1, 2):
-                z_wait(4 * w + i)
-
+        c = ORDER[n]
+        if c < 4:
+            slots = [4 * c + i for i in range(4 if c == 3 else 3)]
+        else:
+            slots = [4 * c + i for i in (1, 2, 3)]
+        for slot in slots:
+            z_wait(slot)
         rows = [zbuf[4 * c + i].astype(F32) for i in range(PER)]
         xall[c, ep] = jnp.concatenate(rows, axis=0).astype(BF16)
 
@@ -183,29 +201,27 @@
             wait(c, colour, 2, 2)
             share(c, colour, 2, 2)
 
-    rows256 = NE * 2 * PER
-
     def compute(n):
-        c, _, _ = chunk_of(n)
+        c = chunk_of(n)
+
+        @pl.when(n == 0)
+        def _():
+            loads[3].wait()
+            loads[4].wait()
+
         half = xall.at[c, pl.ds(0, NE // 2)]
         pltpu.make_async_copy(half, half, d_sem.at[c]).wait()
         gates = xall[c, :, :, pl.ds(model, 128)].reshape(rows256, 128)
-        e_at = lax.broadcasted_iota(jnp.int32, (128, width), 0)
-        f_at = lax.broadcasted_iota(jnp.int32, (128, width), 1)
-        pick = jnp.where(e_at == experts * ep + f_at // part, 1.0, 0.0).astype(BF16)
-        gate = jnp.dot(gates, pick, preferred_element_type=F32)
+        gate = jnp.dot(gates, pick_ref[...], preferred_element_type=F32)
         live = gate > 0
-        r_at = lax.broadcasted_iota(jnp.int32, (rows256, rows256), 0)
-        c_at = lax.broadcasted_iota(jnp.int32, (rows256, rows256), 1)
-        earlier = ((r_at % 8) // 2 == (c_at % 8) // 2) & (c_at < r_at)
-        slot = jnp.dot(
-            jnp.where(earlier, 1.0, 0.0).astype(BF16), jnp.where(live, 1.0, 0.0).astype(BF16),
-            preferred_element_type=F32,
-        )
+        slot = jnp.dot(earlier_ref[...], jnp.where(live, 1.0, 0.0).astype(BF16), preferred_element_type=F32)
         slot = jnp.where(live, slot, -1.0).reshape(NE, 8, width)
         rows = xall[c, :, :, pl.ds(0, model)].reshape(rows256, model)
         grad_in = lax.dot_general(rows, w_ref[...], (((1,), (1,)), ((), ())), preferred_element_type=F32)
-        own_group = [hid_ref[group_of(n, i)].astype(F32) for i in range(PER)]
+        own_group = []
+        for i in range(PER):
+            h = hid_ref[group_of(c, i)].astype(F32)
+            own_group.append(jnp.concatenate([h[:, j, :] for j in range(experts)], axis=1))
         row8 = lax.broadcasted_iota(jnp.int32, (8, width), 0) // 2
         hid = jnp.zeros((NE, 8, width), F32)
         for s in range(capacity):
@@ -215,18 +231,11 @@
             hid = jnp.where(slot == float(s), wide[None], hid)
         grad3 = grad_in.reshape(NE, 8, width)
         gate3 = gate.reshape(NE, 8, width)
-        out = (gate3 * grad3).astype(BF16).astype(F32)
         term = hid * grad3
         terms = []
-        outs = []
         for s in range(capacity):
-            here = slot == float(s)
-            o = jnp.sum(jnp.where(here, out, 0.0), axis=0)
-            t = jnp.sum(jnp.where(here, term, 0.0), axis=0)
-            outs.append(o + pltpu.roll(o, 7, 0))
+            t = jnp.sum(jnp.where(slot == float(s), term, 0.0), axis=0)
             terms.append(t + pltpu.roll(t, 7, 0))
-        for i in range(PER):
-            hg_ref[group_of(n, i)] = jnp.concatenate([o[2 * i : 2 * i + 1] for o in outs], axis=0)
         t = jnp.concatenate(terms, axis=0)
         hi = t.astype(BF16)
         rest = t - hi.astype(F32)
@@ -241,46 +250,66 @@
             lanes = lanes + pltpu.roll(sums[8 * s : 8 * s + 8], experts * s, 1)
         for i in range(PER):
             msg[4 * c + i] = lanes[2 * i : 2 * i + 1]
+        out = (gate3 * grad3).astype(BF16).astype(F32)
+        outs = []
+        for s in range(capacity):
+            o = jnp.sum(jnp.where(slot == float(s), out, 0.0), axis=0)
+            outs.append(o + pltpu.roll(o, 7, 0))
+        for i in range(PER):
+            o = jnp.concatenate([o[2 * i : 2 * i + 1] for o in outs], axis=0)
+            o = jnp.stack([o[:, j * part : (j + 1) * part] for j in range(experts)], axis=1)
+            hg_ref[group_of(c, i)] = o.astype(BF16)
         weighted = (gate3 * hid).reshape(rows256, width).T.astype(BF16)
+        for i in range(PER):
+            def put(i=i):
+                pltpu.make_async_remote_copy(
+                    src_ref=msg.at[4 * c + i], dst_ref=rbuf.at[4 * c + i],
+                    send_sem=ms_sem.at[0], recv_sem=mr_sem.at[0],
+                    device_id=(group_of(c, i), ep), device_id_type=MESH,
+                ).start()
+            if i == 0:
+                pl.when(n > 0)(put)
+
+                @pl.when(n == 0)
+                def _():
+                    rbuf[16] = msg[16]
+            else:
+                put()
         step = 512
         for m in range(model // step):
             cols = pl.ds(m * step, step)
             piece = xall[c, :, :, cols].reshape(rows256, step)
             dwacc[:, cols] += jnp.dot(weighted, piece, preferred_element_type=F32)
-        for i in range(PER):
-            def put(i=i):
-                pltpu.make_async_remote_copy(
-                    src_ref=msg.at[4 * c + i], dst_ref=rbuf.at[4 * c + i],
-                    send_sem=ms_sem.at[0], recv_sem=mr_sem.at[0],
-                    device_id=(group_of(n, i), ep), device_id_type=MESH,
-                ).start()
-            if i == 0:
-                pl.when(n > 0)(put)
-
-                @pl.when(n == 0)
-                def _():
-                    rbuf[16] = msg[16]
-            else:
-                put()
 
     fetch(0)
+    forward(0)
 
     def step(n, carry):
-        for back, stage in enumerate((stage1, stage2, stage3, stage4, stage5)):
+        def run(back, stage):
             @pl.when((n >= back) & (n < CHUNKS + back))
-            def _(back=back, stage=stage):
-                stage(chunk_of(n - back)[0])
-
-        @pl.when(n < CHUNKS - 1)
+            def _():
+                stage(chunk_of(n - back))
+
+        run(0, stage1)
+        run(1, stage2)
+        run(4, stage5)
+        run(2, stage3)
+        run(3, stage4)
+
+        for i in range(CHUNKS - 1):
+            @pl.when(n == i)
+            def _(i=i):
+                fetch(i + 1)
+                if i in (1, 2):
+                    forward(i)
+
+        @pl.when(n >= 4)
         def _():
-            fetch(n + 1)
-
-        @pl.when(n >= 5)
-        def _():
-            compute(n - 5)
+            compute(n - 4)
+
         return carry
 
-    lax.fori_loop(0, CHUNKS + 5, step, 0)
+    lax.fori_loop(0, CHUNKS + 4, step, 0)
     dw_ref[...] = dwacc[...].astype(BF16)
 
     mine = xall[4, :, :, pl.ds(model, 128)].astype(F32).reshape(rows256, 128) > 0
@@ -318,7 +347,13 @@
         for s in range(capacity):
             v = jnp.where(counts[r] == float(s), table[s : s + 1], v)
         vals.append(v)
-    val_ref[...] = jnp.concatenate(vals, axis=0)
+    val = jnp.concatenate(vals, axis=0)
+    k_lane = lax.broadcasted_iota(jnp.int32, (2, 8), 1)
+    gg = jnp.zeros((2, 8), F32)
+    for k in range(ids.shape[1]):
+        one = jnp.sum(jnp.where(e_lane == ids[:, k : k + 1], val, 0.0), axis=1, keepdims=True)
+        gg = jnp.where(k_lane == k, one, gg)
+    gg_ref[...] = gg
 
     sent = zbuf.at[pl.ds(0, NZ - 1)]
     pltpu.make_async_copy(sent, sent, zs_sem.at[0]).wait()
@@ -335,19 +370,17 @@
     groups, experts, capacity, part = hidden.shape
     model = out_grad.shape[1]
     width = experts * part
-    named = expert_ids[:, :, None] == jnp.arange(128, dtype=jnp.int32)[None, None, :]
-    gates = jnp.sum(jnp.where(named, gate_values[:, :, None], 0.0), axis=1)
-    own = jnp.concatenate([out_grad, gates.astype(BF16)], axis=1)
-    hid = jnp.transpose(hidden, (0, 2, 1, 3)).reshape(groups, capacity, width)
+    width = experts * part
     vmem = pl.BlockSpec(memory_space=pltpu.VMEM)
-    hid_grad, weight_grad, values = pl.pallas_call(
+    hbm = pl.BlockSpec(memory_space=pltpu.HBM)
+    hid_grad, weight_grad, gate_grad = pl.pallas_call(
         kernel,
         out_shape=(
-            jax.ShapeDtypeStruct((groups, capacity, width), F32),
+            jax.ShapeDtypeStruct((groups, capacity, experts, part), BF16),
             jax.ShapeDtypeStruct((width, model), BF16),
-            jax.ShapeDtypeStruct((2, 128), F32),
+            jax.ShapeDtypeStruct((2, 8), F32),
         ),
-        in_specs=[vmem] * 3,
+        in_specs=[hbm] * 5,
         out_specs=(vmem,) * 3,
         scratch_shapes=[
             pltpu.VMEM((NZ, 2, LANES), BF16),
@@ -356,6 +389,12 @@
             pltpu.VMEM((NZ, 1, 128), F32),
             pltpu.VMEM((NZ, 1, 128), F32),
             pltpu.VMEM((NE, 8, 128), F32),
+            pltpu.VMEM(expert_ids.shape, jnp.int32),
+            pltpu.VMEM(gate_values.shape, F32),
+            pltpu.VMEM((groups, capacity, experts, part), BF16),
+            pltpu.VMEM((width, model), BF16),
+            pltpu.VMEM((128, width), BF16),
+            pltpu.VMEM((NE * 2 * PER, NE * 2 * PER), BF16),
             pltpu.SemaphoreType.DMA((1,)),
             pltpu.SemaphoreType.DMA((NZ,)),
             pltpu.SemaphoreType.DMA((CHUNKS,)),
@@ -365,17 +404,22 @@
             pltpu.SemaphoreType.DMA((1,)),
             pltpu.SemaphoreType.DMA((1,)),
             pltpu.SemaphoreType.DMA((1,)),
+            pltpu.SemaphoreType.DMA((5,)),
         ],
         compiler_params=pltpu.CompilerParams(
-            collective_id=0, has_side_effects=True, vmem_limit_bytes=56 * 1024 * 1024
+            collective_id=0, has_side_effects=True, vmem_limit_bytes=40 * 1024 * 1024
         ),
-    )(own, hid, w_down.reshape(width, model))
-    hid_grad = hid_grad.astype(BF16).reshape(groups, capacity, experts, part)
-    picked = jnp.where(named, values[:, None, :], 0.0)
+    )(*(
+        pltpu.with_memory_space_constraint(one, pltpu.HBM)
+        for one in (
+            out_grad, expert_ids, gate_values,
+            jnp.transpose(hidden, (0, 2, 1, 3)), w_down.reshape(width, model),
+        )
+    ))
     return (
         jnp.transpose(hid_grad, (0, 2, 1, 3)),
         weight_grad.reshape(experts, part, model),
-        jnp.sum(picked, axis=2),
+        gate_grad,
     )
 
 

time: 117 us -> 103 us (0.88)
  Pallas kernels: 108 us -> 99.9 us
  other arithmetic: 4.62 us -> 0 us
  local copies, waits for them, and re-layouts: 3.83 us -> 2.33 us
    pallas_call x1, Pallas kernels: 108 us -> 99.9 us  [per_device(): pl.pallas_call(kernel, out_shape=(jax.ShapeDtypeStruct((groups, capacity,...]
    reduce_sum x2 -> x0, other arithmetic: 2.22 us -> none  [the longest x1 1.39 us: per_device(): jnp.sum(picked, axis=2)]
    reshape x2 -> x0, local copies, waits for them, and re-layouts: 1.95 us -> none  [the longest x1 1.8 us: per_device(): hid = jnp.transpose(hidden, (0, 2, 1, 3)).reshape(groups, capacity, width)]
    concatenate x1 -> x0, other arithmetic: 1.33 us -> none  [per_device(): own = jnp.concatenate([out_grad, gates.astype(BF16)], axis=1)]
where the time goes in v2:
time: 103 us
  Pallas kernels  99.9 us (97%)
  local copies, waits for them, and re-layouts  2.33 us (2%)
    pallas_call x1, Pallas kernels, per_device(): pl.pallas_call(kernel, out_shape=(jax.ShapeDtypeStruct((groups, capacity,...  99.9 us
    unnamed x3, local copies, waits for them, and re-layouts  2.33 us

profile of v2, /device:TPU:1, one launch (start us, length us, event | category | flops | bytes accessed | tf_op | source)
XLA Modules:
  0.0 102.9 jit_solution(5197302871157512192)
XLA Ops:
  0.6 99.9 %shard_map.76 = (bf16[32,7,4,48]{3,2,1,0:T(4,128)(2,1)S(1)}, bf16[192,3584]{1,0:T(8,128)(2,1)S(1)}, f32[2,8]{1,0:T(2,128)S(1)}) custom-call(bf16[2,3584]{1,0:T(2,128)(2,1)} %rows_hbm.1, s32[2,8]{1,0:T(2,128)} %ids_hbm.1, f32[2,8]{1,0:T(2,128)} %gates_hbm.1, bf16[32,7,4,48]{3,2,1,0:T(4,128)(2,1)} %bitcast.7, bf16[192,3584]{1,0:T(8,128)(2,1)} %bitcast.6), custom_call_target="tpu_custom_call" | custom-call | tf_op jit(solution)/shard_map/pallas_call | solution.py:376
  100.5 0.7 copy.11
  101.2 1.1 %copy.12 = bf16[4,48,3584]{2,1,0:T(8,128)(2,1)} copy(bf16[4,48,3584]{2,1,0:T(8,128)(2,1)S(1)} %bitcast.4) | data formatting | bytes 2752512
  102.3 0.6 copy.13
